TPU v7x, 32 devices: a whole 2x2x4 slice. The times are simulated.
32 devices in a mesh: head: 8 (over z, x), client: 4 (over y, core).
Axes of the slice: x: 2, y: 2, z: 4, core: 2. Of those that a mesh axis runs over, the one named last changes fastest.
Arguments:
- client_ids: int32 [32], replicated, may hold values from 0 to 127, as said below
- client_table: bfloat16 [128, 256], replicated, may hold values from -6 to 6
- in_weight: bfloat16 [256, 4096], P(None, 'client'), may hold values from -0.375 to 0.375
- in_bias: float32 [4096], P('client'), may hold values from -3 to 3
- head_weight: bfloat16 [4096, 131072], P('client', 'head'), may hold values from -0.09375 to 0.09375
- tokens: int32 [32, 256], P(('head', 'client')), may hold values from 0 to 255
- labels: int32 [32, 256], P(('head', 'client')), may hold values from 0 to 255
- byte_table: bfloat16 [256, 4096], P(None, 'client'), may hold values from -5.5 to 6.7
- out_table: bfloat16 [256, 4096], P(None, 'client'), may hold values from -5.625 to 5.625
Outputs:
- head_grad: bfloat16 [4096, 131072], P('client', 'head')
- in_grad: float32 [256, 4096], P(None, 'client')
- losses: float32 [32], P(('head', 'client'))
Inputs may be any that keep to these rules, and one draw needn't show every extreme that they name: `client_ids`: distinct population indices.
All inputs are finite; a program needn't handle non-finite values.
Results may differ from a plain program's by a relative error of at most 0.0085.
Values may be sent and summed in bfloat16 or wider, within the bound.
A program may use at most 128 MiB of HBM per device.

v0:
```python
import jax
import jax.numpy as jnp
from jax import lax
from jax.sharding import PartitionSpec as P

EPSILON = 1e-06
learn_rate = 0.1


def client_loss(factor_a, factor_b, inputs, label_row, out_table):
    depth = factor_a.shape[0]
    rank_size = factor_a.shape[1]
    normed_in = inputs * lax.rsqrt(jnp.mean(inputs * inputs, -1, keepdims=True) + EPSILON)
    low_rank = jnp.dot(normed_in, factor_a, precision=lax.Precision.HIGHEST)
    adapted = inputs + jnp.dot(low_rank, factor_b, precision=lax.Precision.HIGHEST) / jnp.sqrt(
        jnp.float32(depth * rank_size)
    )
    normed = (adapted * lax.rsqrt(jnp.mean(adapted * adapted, -1, keepdims=True) + EPSILON)).astype(
        jnp.bfloat16
    )
    logits = lax.dot_general(
        normed, out_table, (((1,), (1,)), ((), ())), preferred_element_type=jnp.float32
    )
    logits = logits * (4.0 / jnp.sqrt(jnp.float32(depth)))
    log_total = jax.nn.logsumexp(logits, -1)
    vocab_ids = lax.broadcasted_iota(jnp.int32, logits.shape, 1)
    picked = jnp.sum(jnp.where(vocab_ids == label_row[:, None], logits, 0.0), -1)
    return jnp.sum(log_total - picked)


def train_client(factor_row, token_row, label_row, byte_table, out_table):
    depth = byte_table.shape[1]
    split_at = factor_row.shape[0] // 2
    rank_size = split_at // depth
    start_a = factor_row[:split_at].reshape(depth, rank_size).astype(jnp.float32)
    start_b = factor_row[split_at:].reshape(rank_size, depth).astype(jnp.float32)
    onehot = (
        token_row[:, None]
        == lax.broadcasted_iota(jnp.int32, (token_row.shape[0], byte_table.shape[0]), 1)
    ).astype(jnp.bfloat16)
    inputs = jnp.dot(onehot, byte_table, preferred_element_type=jnp.float32)
    loss_grad = jax.value_and_grad(client_loss, argnums=(0, 1))
    first_loss, (grad_a, grad_b) = loss_grad(start_a, start_b, inputs, label_row, out_table)
    middle_a = start_a - learn_rate * grad_a
    middle_b = start_b - learn_rate * grad_b
    second_loss, (grad_a, grad_b) = loss_grad(middle_a, middle_b, inputs, label_row, out_table)
    final_a = middle_a - learn_rate * grad_a
    final_b = middle_b - learn_rate * grad_b
    deltas = jnp.concatenate(
        [(final_a - start_a).reshape(-1), (final_b - start_b).reshape(-1)]
    ).astype(jnp.bfloat16)
    return (deltas, first_loss / token_row.shape[0])


def local(
    client_ids, client_table, in_weight, in_bias, head_weight, tokens, labels, byte_table, out_table
):
    head_count = lax.axis_size("head")
    group_count = lax.axis_size("client")
    per_device = tokens.shape[0]
    byte_full, out_full = (
        lax.all_gather(byte_table, "client", axis=1, tiled=True),
        lax.all_gather(out_table, "client", axis=1, tiled=True),
    )
    ordered = client_ids.reshape(head_count, group_count, per_device).transpose(1, 0, 2).reshape(-1)
    chosen = client_table[ordered]
    preact = jnp.dot(chosen, in_weight, preferred_element_type=jnp.float32) + in_bias
    hidden = jnp.maximum(preact, 0.0).astype(jnp.bfloat16)
    hidden_rows = hidden
    summed = lax.psum_scatter(
        jnp.dot(hidden_rows, head_weight, preferred_element_type=jnp.float32),
        "client",
        scatter_dimension=0,
        tiled=True,
    )
    owned = lax.all_to_all(
        summed.astype(jnp.bfloat16), "head", split_axis=0, concat_axis=1, tiled=True
    )

    def run_client(record):
        return train_client(record[0], record[1], record[2], byte_full, out_full)

    deltas, losses = lax.map(run_client, (owned, tokens, labels))
    returned = lax.all_to_all(deltas, "head", split_axis=1, concat_axis=0, tiled=True)
    received = lax.all_gather(returned, "client", axis=0, tiled=True)
    hidden_rows = hidden
    grad_sum = lax.dot_general(
        hidden_rows, received, (((0,), (0,)), ((), ())), preferred_element_type=jnp.float32
    )
    partial_value = lax.dot_general(
        received, head_weight, (((1,), (1,)), ((), ())), preferred_element_type=jnp.float32
    )
    hidden_back = partial_value
    grad_sum, hidden_back = (grad_sum, hidden_back)
    hidden_back = lax.psum(hidden_back, "head")
    masked = jnp.where(preact > 0, hidden_back, 0.0)
    in_grad = lax.dot_general(
        chosen.astype(jnp.float32),
        masked,
        (((0,), (0,)), ((), ())),
        precision=lax.Precision.HIGHEST,
    )
    return (grad_sum.astype(jnp.bfloat16), in_grad, losses)


def solution(mesh):
    placed = (
        P(),
        P(),
        P(None, "client"),
        P("client"),
        P("client", "head"),
        P(("head", "client"), None),
        P(("head", "client"), None),
        P(None, "client"),
        P(None, "client"),
    )
    return jax.shard_map(
        local,
        mesh=mesh,
        in_specs=placed,
        out_specs=(P("client", "head"), P(None, "client"), P(("head", "client"))),
        check_vma=False,
    )
```

profile of v0, /device:TPU:0, one launch (start us, length us, event | category | flops | bytes accessed | tf_op | source)
XLA Modules:
  0.0 274.1 jit_solution(7337150185194927193)
XLA Ops:
  7.2 0.8 reshape.166
  8.2 1.5 gather_fusion
  9.7 0.9 convolution_add_fusion
  10.5 14.9 %fusion.59 = f32[32,16384]{1,0:T(8,128)} fusion(bf16[1024,16384]{1,0:T(8,128)(2,1)} %param.13, f32[32,1024]{1,0:T(8,128)S(1)} %convolution_add_fusion), kind=kOutput, calls=%fused_computation.91 | convolution fusion | flops 1073807360 | bytes 35782656 | tf_op jit(solution)/shard_map/dot_general | solution.py:71
  25.5 0.7 all-gather.5.cloned.1.call-update
  26.2 0.7 all-gather.7.cloned.1.call-update
  26.9 32.6 %reduce-scatter.2.cloned.1.call-done = f32[8,16384]{1,0:T(8,128)} async-done(((f32[32,16384]{1,0:T(8,128)}), f32[8,16384]{1,0:T(8,128)}) %reduce-scatter.2.cloned.1.call-update) | async-done | bytes 524304 | tf_op jit(solution)/shard_map/reduce_scatter | solution.py:70
  59.5 1.1 convert_bitcast_fusion
  60.6 0.5 broadcast.217
  61.1 0.8 reduce.4
  61.9 0.9 reshape.181
  62.8 5.5 %all-to-all-start = ((bf16[8,2,8192]{2,1,0:T(2,128)(2,1)}), bf16[8,2,8192]{2,1,0:T(2,128)(2,1)S(1)}, u32[]{:S(2)}, u32[]{:S(2)}) async-start(bf16[8,2,8192]{2,1,0:T(2,128)(2,1)} %reshape.181), calls=%async_computation.1 | async-start | bytes 524288 | tf_op jit(solution)/shard_map/all_to_all | solution.py:76
  68.3 15.3 %all-gather.5.cloned.1.call-done = bf16[256,4096]{1,0:T(8,128)(2,1)} async-done(((bf16[256,1024]{1,0:T(8,128)(2,1)}), bf16[256,4096]{1,0:T(8,128)(2,1)}) %all-gather.5.cloned.1.call-update) | async-done | bytes 2097168 | tf_op jit(solution)/shard_map/all_gather | solution.py:62
  83.7 4.4 %multiply_reduce_fusion.2 = (f32[256]{0:T(256)S(1)}, f32[256,4096]{1,0:T(8,128)}) fusion(bf16[256,4096]{1,0:T(8,128)(2,1)} %all-gather.5.cloned.1.call-done, s32[256]{0:T(256)S(1)} %bitcast.43), kind=kOutput, calls=%fused_computation.34 | convolution fusion | flops 539033344 | bytes 6293504 | tf_op jit(solution)/shard_map/while/body/eval_jaxpr/dot_general | solution.py:41
  88.0 0.8 reshape.182
  88.8 1.2 slice_reduce_fusion
  90.0 0.8 reshape.168
  90.9 0.3 copy.24
  91.2 5.0 %fusion.18 = f32[256,16]{0,1:T(8,128)S(1)} fusion(bf16[4096,16]{1,0:T(8,128)(2,1)S(1)} %reshape.168, f32[256,4096]{1,0:T(8,128)} %get-tuple-element.34, f32[256]{0:T(256)S(1)} %add_rsqrt_fusion), kind=kOutput, calls=%fused_computation.39 | convolution fusion | flops 202375168 | bytes 4342784 | tf_op jit(solution)/shard_map/while/body/eval_jaxpr/jvp()/dot_general | solution.py:14
  96.3 4.3 %multiply_reduce_fusion.1 = (f32[256]{0:T(256)S(1)}, f32[256,4096]{1,0:T(8,128)}) fusion(f32[256,4096]{1,0:T(8,128)S(1)} %copy-done.2, f32[256,16]{0,1:T(8,128)S(1)} %fusion.18, bf16[16,4096]{1,0:T(8,128)(2,1)S(1)} %reshape.169), kind=kOutput, calls=%fused_computation.33 | convolution fusion | flops 205520640 | bytes 8537088 | tf_op jit(solution)/shard_map/while/body/eval_jaxpr/jvp()/dot_general | solution.py:15
  100.6 7.2 %all-gather.7.cloned.1.call-done = bf16[256,4096]{1,0:T(8,128)(2,1)} async-done(((bf16[256,1024]{1,0:T(8,128)(2,1)}), bf16[256,4096]{1,0:T(8,128)(2,1)}) %all-gather.7.cloned.1.call-update) | async-done | bytes 2097168 | tf_op jit(solution)/shard_map/all_gather | solution.py:63
  107.8 3.9 %fusion.78 = (f32[256]{0:T(256)S(1)}, f32[256,256]{0,1:T(8,128)S(1)}) fusion(bf16[256,4096]{1,0:T(8,128)(2,1)} %all-gather.7.cloned.1.call-done, f32[256,4096]{1,0:T(8,128)} %get-tuple-element.36, f32[256]{0:T(256)S(1)} %fusion.60), kind=kOutput, calls=%fused_computation.118 | convolution fusion | flops 539098880 | bytes 6555648 | tf_op jit(solution)/shard_map/while/body/eval_jaxpr/jvp()/dot_general | solution.py:21
  111.8 0.6 subtract_reduce_fusion
  112.5 0.9 fusion.10
  113.5 2.8 %fusion.76 = f32[256,16]{0,1:T(8,128)S(1)} fusion(bf16[16,4096]{1,0:T(8,128)(2,1)S(1)} %reshape.169, bf16[256,4096]{1,0:T(8,128)(2,1)S(1)} %get-tuple-element.40, f32[256,4096]{1,0:T(8,128)S(1)} %copy-done.4, f32[256]{0:T(256)S(1)} %multiply_multiply_fusion.1, f32[256]{0:T(256)S(1)} %fusion.60), kind=kOutput, calls=%fused_computation.117 | convolution fusion | flops 207618048 | bytes 6440960 | tf_op jit(solution)/shard_map/while/body/eval_jaxpr/transpose(jvp())/dot_general | solution.py:15
  116.3 3.1 %fusion.6 = f32[16,4096]{1,0:T(8,128)S(1)} fusion(f32[256,16]{0,1:T(8,128)S(1)} %fusion.18, bf16[16,4096]{1,0:T(8,128)(2,1)S(1)} %reshape.169, bf16[256,4096]{1,0:T(8,128)(2,1)S(1)} %get-tuple-element.40, f32[256,4096]{1,0:T(8,128)S(1)} %copy-done.4, f32[256]{0:T(256)S(1)} %multiply_multiply_fusion.1, f32[256]{0:T(256)S(1)} %fusion.60), kind=kOutput, calls=%fused_computation.21 | convolution fusion | flops 207814656 | bytes 6703104 | tf_op jit(solution)/shard_map/while/body/eval_jaxpr/transpose(jvp())/dot_general | solution.py:15
  119.4 2.5 fusion.7
  121.9 3.4 %fusion.15 = f32[256,16]{0,1:T(8,128)S(1)} fusion(f32[4096,16]{0,1:T(8,128)S(1)} %fusion.7, f32[256,4096]{1,0:T(8,128)S(1)} %copy-done.3, f32[256]{0:T(256)S(1)} %add_rsqrt_fusion), kind=kOutput, calls=%fused_computation.36 | convolution fusion | flops 202375168 | bytes 4473856 | tf_op jit(solution)/shard_map/while/body/eval_jaxpr/jvp()/dot_general | solution.py:14
  125.4 4.1 %multiply_reduce_fusion = (f32[256]{0:T(256)S(1)}, f32[256,4096]{1,0:T(8,128)S(1)}) fusion(f32[256,4096]{1,0:T(8,128)S(1)} %copy-done.3, f32[256,16]{0,1:T(8,128)S(1)} %fusion.15, f32[16,4096]{1,0:T(8,128)S(1)} %fusion.6), kind=kOutput, calls=%fused_computation.31 | convolution fusion | flops 205520640 | bytes 8668160 | tf_op jit(solution)/shard_map/while/body/eval_jaxpr/jvp()/dot_general | solution.py:15
  129.5 0.9 fusion.79
  130.4 0.9 fusion.11
  131.4 4.2 %fusion.73 = f32[256,16]{0,1:T(8,128)S(1)} fusion(f32[16,4096]{1,0:T(8,128)S(1)} %fusion.6, bf16[256,4096]{1,0:T(8,128)(2,1)S(1)} %get-tuple-element.46, f32[256,4096]{1,0:T(8,128)S(1)} %get-tuple-element.42, f32[256]{0:T(256)S(1)} %multiply_multiply_fusion, f32[256]{0:T(256)S(1)} %fusion.61), kind=kOutput, calls=%fused_computation.116 | convolution fusion | flops 207618048 | bytes 6572032 | tf_op jit(solution)/shard_map/while/body/eval_jaxpr/transpose(jvp())/dot_general | solution.py:15
  135.6 2.9 %fusion.9 = bf16[16,4096]{1,0:T(8,128)(2,1)S(1)} fusion(f32[16,4096]{1,0:T(8,128)S(1)} %fusion.6, f32[256,16]{0,1:T(8,128)S(1)} %fusion.15, bf16[16,4096]{1,0:T(8,128)(2,1)S(1)} %reshape.169, bf16[256,4096]{1,0:T(8,128)(2,1)S(1)} %get-tuple-element.46, f32[256,4096]{1,0:T(8,128)S(1)} %get-tuple-element.42, f32[256]{0:T(256)S(1)} %multiply_multiply_fusion, ...), kind=kOutput, calls=%fused_computation.25 | convolution fusion | flops 207945728 | bytes 6834176 | tf_op jit(solution)/shard_map/while/body/eval_jaxpr/transpose(jvp())/dot_general | solution.py:15
  138.5 2.5 fusion.8
  141.0 0.5 copy.25
  141.5 1.2 concatenate.17
  142.7 0.2 concatenate.18
  143.0 0.4 copy.29
  143.4 2.2 reduce.5
  145.7 0.2 reshape.183
  145.8 14.9 %all_to_all.26 = bf16[8,2,8192]{2,1,0:T(2,128)(2,1)S(1)} all-to-all(bf16[8,2,8192]{2,1,0:T(2,128)(2,1)S(1)} %reshape.183), channel_id=1, replica_groups=mesh['head'=8,'client'=4] {'head'}, dimensions={0} | all-to-all | bytes 524288 | tf_op jit(solution)/shard_map/all_to_all | solution.py:84
  160.7 0.3 reshape.184
  161.0 1.0 copy.27
  162.6 14.3 %all-gather.9.cloned.1.call-done = bf16[1,32,16384]{2,1,0:T(8,128)(2,1)} async-done(((bf16[1,8,16384]{2,1,0:T(8,128)(2,1)}), bf16[1,32,16384]{2,1,0:T(8,128)(2,1)}) %all-gather.9.cloned.1.call-update) | async-done | bytes 1048592 | tf_op jit(solution)/shard_map/all_gather | solution.py:85
  177.0 16.1 %fusion.30 = f32[32,1024]{1,0:T(8,128)} fusion(bf16[1024,16384]{1,0:T(8,128)(2,1)} %param.13, bf16[1,32,16384]{2,1,0:T(8,128)(2,1)} %all-gather.9.cloned.1.call-done), kind=kOutput, calls=%fused_computation.52 | convolution fusion | flops 1073741824 | bytes 34734080 | tf_op jit(solution)/shard_map/dot_general | solution.py:90
  193.1 14.9 %convolution_convert_fusion = bf16[1024,16384]{1,0:T(8,128)(2,1)} fusion(bf16[1,32,16384]{2,1,0:T(8,128)(2,1)S(1)} %copy-done.6, f32[32,1024]{1,0:T(8,128)S(1)} %convolution_add_fusion), kind=kOutput, calls=%fused_computation.1 | convolution fusion | flops 1090584576 | bytes 34734080 | tf_op jit(solution)/shard_map/dot_general | solution.py:87
  207.9 55.7 %all-reduce.2.cloned.1.call-done = f32[32,1024]{1,0:T(8,128)} async-done(((f32[32,1024]{1,0:T(8,128)}), f32[32,1024]{1,0:T(8,128)}) %all-reduce.2.cloned.1.call-update) | async-done | bytes 131088 | tf_op jit(solution)/shard_map/psum | solution.py:95
  263.7 2.5 fusion.42
  (43 shorter events, 1.1 us)
Async XLA Ops:
  7.2 2.5 copy-start
  7.2 52.3 %reduce-scatter.2.cloned.1.call-start = ((), (), s32[]{:S(2)}) async-start(), calls=%async_computation.3 | async-start | bytes 2621440 | tf_op jit(solution)/shard_map/reduce_scatter | solution.py:70
  25.4 58.2 %copy-start.7 = (s32[1,256]{1,0:T(1,128)S(1)}, s32[1,256]{1,0:T(1,128)}, u32[]{:S(2)}) copy-start(s32[1,256]{1,0:T(1,128)} %param.14) | copy-start | bytes 3076
  25.4 58.2 %all-gather.5.cloned.1.call-start = ((), (), s32[]{:S(2)}) async-start(), calls=%async_computation.4 | async-start | bytes 2621440 | tf_op jit(solution)/shard_map/all_gather | solution.py:62
  26.2 81.6 %all-gather.7.cloned.1.call-start = ((), (), s32[]{:S(2)}) async-start(), calls=%async_computation.5 | async-start | bytes 2621440 | tf_op jit(solution)/shard_map/all_gather | solution.py:63
  62.8 25.2 %all-to-all-start = ((bf16[8,2,8192]{2,1,0:T(2,128)(2,1)}), bf16[8,2,8192]{2,1,0:T(2,128)(2,1)S(1)}, u32[]{:S(2)}, u32[]{:S(2)}) async-start(bf16[8,2,8192]{2,1,0:T(2,128)(2,1)} %reshape.181), calls=%async_computation.1 | async-start | bytes 524288 | tf_op jit(solution)/shard_map/all_to_all | solution.py:76
  68.3 108.7 %all-gather.9.cloned.1.call-start = ((), (), s32[]{:S(2)}) async-start(), calls=%async_computation.7 | async-start | bytes 1310720 | tf_op jit(solution)/shard_map/all_gather | solution.py:85
  91.2 5.1 %copy-start.2 = (f32[256,4096]{1,0:T(8,128)S(1)}, f32[256,4096]{1,0:T(8,128)}, u32[]{:S(2)}) copy-start(f32[256,4096]{1,0:T(8,128)} %get-tuple-element.34) | copy-start | bytes 12582916
  100.6 11.1 %copy-start.8 = (s32[1,256]{1,0:T(1,128)S(1)}, s32[1,256]{1,0:T(1,128)}, u32[]{:S(2)}) copy-start(s32[1,256]{1,0:T(1,128)} %param.15) | copy-start | bytes 3076
  107.8 4.6 %copy-start.4 = (f32[256,4096]{1,0:T(8,128)S(1)}, f32[256,4096]{1,0:T(8,128)}, u32[]{:S(2)}) copy-start(f32[256,4096]{1,0:T(8,128)} %get-tuple-element.36) | copy-start | bytes 12582916
  107.8 4.7 %copy-start.5 = (bf16[256,4096]{1,0:T(8,128)(2,1)S(1)}, bf16[256,4096]{1,0:T(8,128)(2,1)}, u32[]{:S(2)}) copy-start(bf16[256,4096]{1,0:T(8,128)(2,1)} %all-gather.7.cloned.1.call-done) | copy-start | bytes 6291460
  116.3 3.1 %copy-start.3 = (f32[256,4096]{1,0:T(8,128)S(1)}, f32[256,4096]{1,0:T(8,128)}, u32[]{:S(2)}) copy-start(f32[256,4096]{1,0:T(8,128)} %get-tuple-element.34) | copy-start | bytes 12582916
  162.0 101.7 %all-reduce.2.cloned.1.call-start = ((), (), s32[]{:S(2)}) async-start(), calls=%async_computation.6 | async-start | bytes 262144 | tf_op jit(solution)/shard_map/psum | solution.py:95
  177.0 16.1 %copy-start.6 = (bf16[1,32,16384]{2,1,0:T(8,128)(2,1)S(1)}, bf16[1,32,16384]{2,1,0:T(8,128)(2,1)}, u32[]{:S(2)}) copy-start(bf16[1,32,16384]{2,1,0:T(8,128)(2,1)} %all-gather.9.cloned.1.call-done) | copy-start | bytes 3145732
  193.1 73.1 %copy-start.1 = (bf16[256,1024]{1,0:T(8,128)(2,1)S(1)}, bf16[256,1024]{1,0:T(8,128)(2,1)}, u32[]{:S(2)}) copy-start(bf16[256,1024]{1,0:T(8,128)(2,1)} %param.11) | copy-start | bytes 1572868
Sparse Core Ops, SparseCore 0:
  25.6 33.9 reduce-scatter.1
  61.1 22.5 all-gather.4
  85.2 22.5 all-gather.6
  162.1 14.7 all-gather.8
  193.2 70.4 all-reduce.1
where the time goes:
time: 278 us; the launch traced here: 274 us
  waiting for transfers between devices  127 us (46%)
  matrix products  95 us (34%)
  between operations  15.9 us (6%)
  blocking collectives  14.9 us (5%)
  local copies, waits for them, and re-layouts  10.8 us (4%)
  starting transfers between devices  5.69 us (2%)
  other arithmetic  5.08 us (2%)
    psum x1, waiting for transfers between devices, local(): hidden_back = lax.psum(hidden_back, 'head')  55.7 us
    reduce_scatter x1, waiting for transfers between devices, local(): lax.psum_scatter(jnp.dot(hidden_rows, head_weight, preferred_element_type...  32.6 us
    dot_general x6, matrix products, client_loss(): jnp.dot(low_rank, factor_b, precision=lax.Precision.HIGHEST)  21.5 us
    dot_general x1, matrix products, local(): lax.dot_general(received, head_weight, (((1,), (1,)), ((), ())), preferre...  16.1 us
    all_gather x1, waiting for transfers between devices, local(): lax.all_gather(byte_table, 'client', axis=1, tiled=True)  15.3 us
    all_to_all x1, blocking collectives, local(): lax.all_to_all(deltas, 'head', split_axis=1, concat_axis=0, tiled=True)  14.9 us
    dot_general x1, matrix products, local(): lax.dot_general(hidden_rows, received, (((0,), (0,)), ((), ())), preferre...  14.9 us
    dot_general x1, matrix products, local(): jnp.dot(hidden_rows, head_weight, preferred_element_type=jnp.float32)  14.9 us
  transfers between devices with their start and end apart: 6, of which 5 were waited for; matrix products, arithmetic and copies ran while one was open for 13% of the time, Pallas kernels for 0%

commit v1 on v0

--- a/solution.py
+++ b/solution.py
@@ -81,7 +81,18 @@
         return train_client(record[0], record[1], record[2], byte_full, out_full)
 
     deltas, losses = lax.map(run_client, (owned, tokens, labels))
-    returned = lax.all_to_all(deltas, "head", split_axis=1, concat_axis=0, tiled=True)
+    e_next, raw_out = (lax.axis_size("head"), lax.axis_index("head"))
+    parts_out = deltas.shape[1] // e_next
+    even = list(deltas.shape)
+    even[1] = parts_out
+    res = even[0]
+    even[0] = res * e_next
+    returned = jnp.zeros(even, deltas.dtype)
+    for pp in range(e_next):
+        later = lax.dynamic_slice_in_dim(deltas, (raw_out ^ pp) * parts_out, parts_out, axis=1)
+        if pp:
+            later = lax.ppermute(later, axis_name="head", perm=[(s, s ^ pp) for s in range(e_next)])
+        returned = lax.dynamic_update_slice_in_dim(returned, later, (raw_out ^ pp) * res, axis=0)
     received = lax.all_gather(returned, "client", axis=0, tiled=True)
     hidden_rows = hidden
     grad_sum = lax.dot_general(

time: 278 us -> 282 us (1.014)
  blocking collectives: 14.9 us -> 0 us
  starting transfers between devices: 5.69 us -> 17.2 us
  local copies, waits for them, and re-layouts: 10.8 us -> 18.8 us
    all_to_all x1 -> x0, blocking collectives: 14.9 us -> none  [local(): lax.all_to_all(deltas, 'head', split_axis=1, concat_axis=0, tiled=True)]
    ppermute x0 -> x7, starting transfers between devices: none -> 11.5 us  [local(): lax.ppermute(later, axis_name='head', perm=[(s, s ^ pp) for s in range(e_...]
    dynamic_update_slice x0 -> x8, local copies, waits for them, and re-layouts: none -> 9.35 us  [local(): lax.dynamic_update_slice_in_dim(returned, later, (raw_out ^ pp) * res, ax...]
  transfers between devices with their start and end apart: 6 -> 13, of which waited for: 5 -> 5; matrix products, arithmetic and copies ran while one was open for 13% -> 16% of each run, Pallas kernels for 0% -> 0%
where the time goes in v1:
time: 282 us; the launch traced here: 278 us
  waiting for transfers between devices  128 us (45%)
  matrix products  95 us (34%)
  local copies, waits for them, and re-layouts  18.8 us (7%)
  starting transfers between devices  17.2 us (6%)
  between operations  16.2 us (6%)
    psum x1, waiting for transfers between devices, local(): hidden_back = lax.psum(hidden_back, 'head')  55.7 us
    reduce_scatter x1, waiting for transfers between devices, local(): lax.psum_scatter(jnp.dot(hidden_rows, head_weight, preferred_element_type...  32.5 us
    dot_general x6, matrix products, client_loss(): jnp.dot(low_rank, factor_b, precision=lax.Precision.HIGHEST)  21.5 us
    all_gather x1, waiting for transfers between devices, local(): received = lax.all_gather(returned, 'client', axis=0, tiled=True)  16.2 us
    dot_general x1, matrix products, local(): lax.dot_general(received, head_weight, (((1,), (1,)), ((), ())), preferre...  16.1 us
    all_gather x1, waiting for transfers between devices, local(): lax.all_gather(byte_table, 'client', axis=1, tiled=True)  15.3 us
    dot_general x1, matrix products, local(): lax.dot_general(hidden_rows, received, (((0,), (0,)), ((), ())), preferre...  14.9 us
    dot_general x1, matrix products, local(): jnp.dot(hidden_rows, head_weight, preferred_element_type=jnp.float32)  14.9 us
  transfers between devices with their start and end apart: 13, of which 5 were waited for; matrix products, arithmetic and copies ran while one was open for 16% of the time, Pallas kernels for 0%

profile of v1, /device:TPU:0, one launch (start us, length us, event | category | flops | bytes accessed | tf_op | source)
XLA Modules:
  0.0 278.4 jit_solution(8159362830154557964)
XLA Ops:
  7.2 0.8 reshape.137
  8.2 1.5 gather_fusion
  9.7 0.9 convolution_add_fusion
  10.5 14.9 %fusion.57 = f32[32,16384]{1,0:T(8,128)} fusion(bf16[1024,16384]{1,0:T(8,128)(2,1)} %param.13, f32[32,1024]{1,0:T(8,128)S(1)} %convolution_add_fusion), kind=kOutput, calls=%fused_computation.88 | convolution fusion | flops 1073807360 | bytes 35782656 | tf_op jit(solution)/shard_map/dot_general | solution.py:71
  25.5 0.7 all-gather.4.cloned.1.call-update
  27.0 32.5 %reduce-scatter.2.cloned.1.call-done = f32[8,16384]{1,0:T(8,128)} async-done(((f32[32,16384]{1,0:T(8,128)}), f32[8,16384]{1,0:T(8,128)}) %reduce-scatter.2.cloned.1.call-update) | async-done | bytes 524304 | tf_op jit(solution)/shard_map/reduce_scatter | solution.py:70
  59.5 1.1 convert_bitcast_fusion
  61.1 0.8 reduce.4
  61.9 0.9 reshape.153
  62.8 5.5 %all-to-all-start = ((bf16[8,2,8192]{2,1,0:T(2,128)(2,1)}), bf16[8,2,8192]{2,1,0:T(2,128)(2,1)S(1)}, u32[]{:S(2)}, u32[]{:S(2)}) async-start(bf16[8,2,8192]{2,1,0:T(2,128)(2,1)} %reshape.153), calls=%async_computation.1 | async-start | bytes 524288 | tf_op jit(solution)/shard_map/all_to_all | solution.py:76
  68.3 15.3 %all-gather.4.cloned.1.call-done = bf16[256,4096]{1,0:T(8,128)(2,1)} async-done(((bf16[256,1024]{1,0:T(8,128)(2,1)}), bf16[256,4096]{1,0:T(8,128)(2,1)}) %all-gather.4.cloned.1.call-update) | async-done | bytes 2097168 | tf_op jit(solution)/shard_map/all_gather | solution.py:62
  83.7 4.4 %multiply_reduce_fusion.2 = (f32[256]{0:T(256)S(1)}, f32[256,4096]{1,0:T(8,128)}) fusion(bf16[256,4096]{1,0:T(8,128)(2,1)} %all-gather.4.cloned.1.call-done, s32[256]{0:T(256)S(1)} %bitcast.38), kind=kOutput, calls=%fused_computation.34 | convolution fusion | flops 539033344 | bytes 6293504 | tf_op jit(solution)/shard_map/while/body/eval_jaxpr/dot_general | solution.py:41
  88.0 0.8 reshape.154
  88.8 1.2 slice_reduce_fusion.1
  90.0 0.8 reshape.139
  91.2 5.0 %fusion.18 = f32[256,16]{0,1:T(8,128)S(1)} fusion(bf16[4096,16]{1,0:T(8,128)(2,1)S(1)} %reshape.139, f32[256,4096]{1,0:T(8,128)} %get-tuple-element.42, f32[256]{0:T(256)S(1)} %add_rsqrt_fusion), kind=kOutput, calls=%fused_computation.39 | convolution fusion | flops 202375168 | bytes 4342784 | tf_op jit(solution)/shard_map/while/body/eval_jaxpr/jvp()/dot_general | solution.py:14
  96.3 4.3 %multiply_reduce_fusion.1 = (f32[256]{0:T(256)S(1)}, f32[256,4096]{1,0:T(8,128)}) fusion(f32[256,4096]{1,0:T(8,128)S(1)} %copy-done.2, f32[256,16]{0,1:T(8,128)S(1)} %fusion.18, bf16[16,4096]{1,0:T(8,128)(2,1)S(1)} %reshape.140), kind=kOutput, calls=%fused_computation.33 | convolution fusion | flops 205520640 | bytes 8537088 | tf_op jit(solution)/shard_map/while/body/eval_jaxpr/jvp()/dot_general | solution.py:15
  100.6 7.2 %all-gather.6.cloned.1.call-done = bf16[256,4096]{1,0:T(8,128)(2,1)} async-done(((bf16[256,1024]{1,0:T(8,128)(2,1)}), bf16[256,4096]{1,0:T(8,128)(2,1)}) %all-gather.6.cloned.1.call-update) | async-done | bytes 2097168 | tf_op jit(solution)/shard_map/all_gather | solution.py:63
  107.8 3.9 %fusion.77 = (f32[256]{0:T(256)S(1)}, f32[256,256]{0,1:T(8,128)S(1)}) fusion(bf16[256,4096]{1,0:T(8,128)(2,1)} %all-gather.6.cloned.1.call-done, f32[256,4096]{1,0:T(8,128)} %get-tuple-element.44, f32[256]{0:T(256)S(1)} %fusion.58), kind=kOutput, calls=%fused_computation.118 | convolution fusion | flops 539098880 | bytes 6555648 | tf_op jit(solution)/shard_map/while/body/eval_jaxpr/jvp()/dot_general | solution.py:21
  112.5 0.9 fusion.10
  113.5 2.8 %fusion.74 = f32[256,16]{0,1:T(8,128)S(1)} fusion(bf16[16,4096]{1,0:T(8,128)(2,1)S(1)} %reshape.140, bf16[256,4096]{1,0:T(8,128)(2,1)S(1)} %get-tuple-element.48, f32[256,4096]{1,0:T(8,128)S(1)} %copy-done.4, f32[256]{0:T(256)S(1)} %multiply_multiply_fusion.1, f32[256]{0:T(256)S(1)} %fusion.58), kind=kOutput, calls=%fused_computation.116 | convolution fusion | flops 207618048 | bytes 6440960 | tf_op jit(solution)/shard_map/while/body/eval_jaxpr/transpose(jvp())/dot_general | solution.py:15
  116.3 3.1 %fusion.6 = f32[16,4096]{1,0:T(8,128)S(1)} fusion(f32[256,16]{0,1:T(8,128)S(1)} %fusion.18, bf16[16,4096]{1,0:T(8,128)(2,1)S(1)} %reshape.140, bf16[256,4096]{1,0:T(8,128)(2,1)S(1)} %get-tuple-element.48, f32[256,4096]{1,0:T(8,128)S(1)} %copy-done.4, f32[256]{0:T(256)S(1)} %multiply_multiply_fusion.1, f32[256]{0:T(256)S(1)} %fusion.58), kind=kOutput, calls=%fused_computation.21 | convolution fusion | flops 207814656 | bytes 6703104 | tf_op jit(solution)/shard_map/while/body/eval_jaxpr/transpose(jvp())/dot_general | solution.py:15
  119.4 2.5 fusion.7
  122.0 3.4 %fusion.15 = f32[256,16]{0,1:T(8,128)S(1)} fusion(f32[4096,16]{0,1:T(8,128)S(1)} %fusion.7, f32[256,4096]{1,0:T(8,128)S(1)} %copy-done.3, f32[256]{0:T(256)S(1)} %add_rsqrt_fusion), kind=kOutput, calls=%fused_computation.36 | convolution fusion | flops 202375168 | bytes 4473856 | tf_op jit(solution)/shard_map/while/body/eval_jaxpr/jvp()/dot_general | solution.py:14
  125.4 4.1 %multiply_reduce_fusion = (f32[256]{0:T(256)S(1)}, f32[256,4096]{1,0:T(8,128)S(1)}) fusion(f32[256,4096]{1,0:T(8,128)S(1)} %copy-done.3, f32[256,16]{0,1:T(8,128)S(1)} %fusion.15, f32[16,4096]{1,0:T(8,128)S(1)} %fusion.6), kind=kOutput, calls=%fused_computation.31 | convolution fusion | flops 205520640 | bytes 8668160 | tf_op jit(solution)/shard_map/while/body/eval_jaxpr/jvp()/dot_general | solution.py:15
  129.5 0.9 fusion.78
  130.4 0.9 fusion.11
  131.4 3.2 %fusion.30 = bf16[2,32,8,128]{3,2,1,0:T(8,128)(2,1)S(1)} fusion(f32[16,4096]{1,0:T(8,128)S(1)} %fusion.6, f32[256,16]{0,1:T(8,128)S(1)} %fusion.15, bf16[16,4096]{1,0:T(8,128)(2,1)S(1)} %reshape.140, bf16[256,4096]{1,0:T(8,128)(2,1)S(1)} %get-tuple-element.54, f32[256,4096]{1,0:T(8,128)S(1)} %get-tuple-element.50, f32[256]{0:T(256)S(1)} %multiply_multiply_fusion, ...), kind=kOutput, calls=%fused_computation.51 | convolution fusion | flops 207945728 | bytes 6834176 | tf_op jit(solution)/shard_map/while/body/eval_jaxpr/transpose(jvp())/dot_general | solution.py:15
  134.5 4.0 %fusion.71 = f32[256,16]{0,1:T(8,128)S(1)} fusion(f32[16,4096]{1,0:T(8,128)S(1)} %fusion.6, bf16[256,4096]{1,0:T(8,128)(2,1)S(1)} %get-tuple-element.54, f32[256,4096]{1,0:T(8,128)S(1)} %get-tuple-element.50, f32[256]{0:T(256)S(1)} %multiply_multiply_fusion, f32[256]{0:T(256)S(1)} %fusion.59), kind=kOutput, calls=%fused_computation.115 | convolution fusion | flops 207618048 | bytes 6572032 | tf_op jit(solution)/shard_map/while/body/eval_jaxpr/transpose(jvp())/dot_general | solution.py:15
  138.5 2.5 fusion.8
  142.4 1.5 collective-permute-start
  144.0 1.6 collective-permute-start.1
  146.2 2.5 collective-permute-start.3
  148.7 1.5 collective-permute-start.4
  150.3 3.4 %collective-permute-start.5 = (bf16[1,16384]{1,0:T(2,128)(2,1)S(1)}, bf16[1,16384]{1,0:T(2,128)(2,1)S(1)}, u32[]{:S(2)}, u32[]{:S(2)}) collective-permute-start(bf16[1,16384]{1,0:T(2,128)(2,1)S(1)} %dynamic_slice.38), channel_id=1, source_target_pairs={{0,24},{4,28},{8,16},{12,20},{16,8},{20,12},{24,0},{28,4},{1,25},{... | collective-permute-start | bytes 98312 | tf_op jit(solution)/shard_map/ppermute | solution.py:94
  154.2 1.1 dynamic_update_slice.30
  155.4 1.1 dynamic_update_slice.31
  156.5 1.1 dynamic_update_slice.32
  157.7 1.1 dynamic_update_slice.33
  158.8 1.1 dynamic_update_slice.34
  160.0 1.1 dynamic_update_slice.35
  161.1 1.4 dynamic_update_slice.36
  162.6 1.1 dynamic_update_slice.37
  165.1 16.2 %all-gather.8.cloned.1.call-done = bf16[32,16384]{1,0:T(8,128)(2,1)} async-done(((bf16[8,16384]{1,0:T(8,128)(2,1)}), bf16[32,16384]{1,0:T(8,128)(2,1)}) %all-gather.8.cloned.1.call-update) | async-done | bytes 1048592 | tf_op jit(solution)/shard_map/all_gather | solution.py:96
  181.3 16.1 %fusion.79 = f32[32,1024]{1,0:T(8,128)} fusion(bf16[32,16384]{1,0:T(8,128)(2,1)} %all-gather.8.cloned.1.call-done, bf16[1024,16384]{1,0:T(8,128)(2,1)} %param.13), kind=kOutput, calls=%fused_computation.120 | convolution fusion | flops 1073741824 | bytes 34734080 | tf_op jit(solution)/shard_map/dot_general | solution.py:101
  197.4 14.9 %convolution_convert_fusion = bf16[1024,16384]{1,0:T(8,128)(2,1)} fusion(bf16[32,16384]{1,0:T(8,128)(2,1)S(1)} %copy-done.6, f32[32,1024]{1,0:T(8,128)S(1)} %convolution_add_fusion), kind=kOutput, calls=%fused_computation.1 | convolution fusion | flops 1090584576 | bytes 34734080 | tf_op jit(solution)/shard_map/dot_general | solution.py:98
  212.3 55.7 %all-reduce.2.cloned.1.call-done = f32[32,1024]{1,0:T(8,128)} async-done(((f32[32,1024]{1,0:T(8,128)}), f32[32,1024]{1,0:T(8,128)}) %all-reduce.2.cloned.1.call-update) | async-done | bytes 131088 | tf_op jit(solution)/shard_map/psum | solution.py:106
  268.0 2.5 fusion.40
  (72 shorter events, 6.5 us)
Async XLA Ops:
  7.2 2.5 copy-start
  7.2 52.3 %reduce-scatter.2.cloned.1.call-start = ((), (), s32[]{:S(2)}) async-start(), calls=%async_computation.2 | async-start | bytes 2621440 | tf_op jit(solution)/shard_map/reduce_scatter | solution.py:70
  25.4 58.2 %copy-start.8 = (s32[1,256]{1,0:T(1,128)S(1)}, s32[1,256]{1,0:T(1,128)}, u32[]{:S(2)}) copy-start(s32[1,256]{1,0:T(1,128)} %param.14) | copy-start | bytes 3076
  25.4 58.2 %all-gather.4.cloned.1.call-start = ((), (), s32[]{:S(2)}) async-start(), calls=%async_computation.3 | async-start | bytes 2621440 | tf_op jit(solution)/shard_map/all_gather | solution.py:62
  26.2 81.6 %all-gather.6.cloned.1.call-start = ((), (), s32[]{:S(2)}) async-start(), calls=%async_computation.4 | async-start | bytes 2621440 | tf_op jit(solution)/shard_map/all_gather | solution.py:63
  62.8 25.2 %all-to-all-start = ((bf16[8,2,8192]{2,1,0:T(2,128)(2,1)}), bf16[8,2,8192]{2,1,0:T(2,128)(2,1)S(1)}, u32[]{:S(2)}, u32[]{:S(2)}) async-start(bf16[8,2,8192]{2,1,0:T(2,128)(2,1)} %reshape.153), calls=%async_computation.1 | async-start | bytes 524288 | tf_op jit(solution)/shard_map/all_to_all | solution.py:76
  68.3 113.0 %all-gather.8.cloned.1.call-start = ((), (), s32[]{:S(2)}) async-start(), calls=%async_computation.5 | async-start | bytes 1310720 | tf_op jit(solution)/shard_map/all_gather | solution.py:96
  91.2 5.1 %copy-start.2 = (f32[256,4096]{1,0:T(8,128)S(1)}, f32[256,4096]{1,0:T(8,128)}, u32[]{:S(2)}) copy-start(f32[256,4096]{1,0:T(8,128)} %get-tuple-element.42) | copy-start | bytes 12582916
  100.6 11.1 %copy-start.9 = (s32[1,256]{1,0:T(1,128)S(1)}, s32[1,256]{1,0:T(1,128)}, u32[]{:S(2)}) copy-start(s32[1,256]{1,0:T(1,128)} %param.15) | copy-start | bytes 3076
  107.8 4.6 %copy-start.4 = (f32[256,4096]{1,0:T(8,128)S(1)}, f32[256,4096]{1,0:T(8,128)}, u32[]{:S(2)}) copy-start(f32[256,4096]{1,0:T(8,128)} %get-tuple-element.44) | copy-start | bytes 12582916
  107.8 4.7 %copy-start.5 = (bf16[256,4096]{1,0:T(8,128)(2,1)S(1)}, bf16[256,4096]{1,0:T(8,128)(2,1)}, u32[]{:S(2)}) copy-start(bf16[256,4096]{1,0:T(8,128)(2,1)} %all-gather.6.cloned.1.call-done) | copy-start | bytes 6291460
  116.3 3.1 %copy-start.3 = (f32[256,4096]{1,0:T(8,128)S(1)}, f32[256,4096]{1,0:T(8,128)}, u32[]{:S(2)}) copy-start(f32[256,4096]{1,0:T(8,128)} %get-tuple-element.42) | copy-start | bytes 12582916
  142.4 7.9 %collective-permute-start = (bf16[1,16384]{1,0:T(2,128)(2,1)S(1)}, bf16[1,16384]{1,0:T(2,128)(2,1)S(1)}, u32[]{:S(2)}, u32[]{:S(2)}) collective-permute-start(bf16[1,16384]{1,0:T(2,128)(2,1)S(1)} %dynamic_slice.33), channel_id=1, source_target_pairs={{0,4},{4,0},{8,12},{12,8},{16,20},{20,16},{24,28},{28,24},{1,5},{5... | collective-permute-start | bytes 98312 | tf_op jit(solution)/shard_map/ppermute | solution.py:94
  144.0 9.7 %collective-permute-start.1 = (bf16[1,16384]{1,0:T(2,128)(2,1)S(1)}, bf16[1,16384]{1,0:T(2,128)(2,1)S(1)}, u32[]{:S(2)}, u32[]{:S(2)}) collective-permute-start(bf16[1,16384]{1,0:T(2,128)(2,1)S(1)} %dynamic_slice.34), channel_id=1, source_target_pairs={{0,8},{4,12},{8,0},{12,4},{16,24},{20,28},{24,16},{28,20},{1,9},{5... | collective-permute-start | bytes 98312 | tf_op jit(solution)/shard_map/ppermute | solution.py:94
  145.5 12.1 %collective-permute-start.2 = (bf16[1,16384]{1,0:T(2,128)(2,1)S(1)}, bf16[1,16384]{1,0:T(2,128)(2,1)S(1)}, u32[]{:S(2)}, u32[]{:S(2)}) collective-permute-start(bf16[1,16384]{1,0:T(2,128)(2,1)S(1)} %dynamic_slice.35), channel_id=1, source_target_pairs={{0,12},{4,8},{8,4},{12,0},{16,28},{20,24},{24,20},{28,16},{1,13},{... | collective-permute-start | bytes 98312 | tf_op jit(solution)/shard_map/ppermute | solution.py:94
  146.2 12.6 %collective-permute-start.3 = (bf16[1,16384]{1,0:T(2,128)(2,1)S(1)}, bf16[1,16384]{1,0:T(2,128)(2,1)S(1)}, u32[]{:S(2)}, u32[]{:S(2)}) collective-permute-start(bf16[1,16384]{1,0:T(2,128)(2,1)S(1)} %dynamic_slice.36), channel_id=1, source_target_pairs={{0,16},{4,20},{8,24},{12,28},{16,0},{20,4},{24,8},{28,12},{1,17},{... | collective-permute-start | bytes 98312 | tf_op jit(solution)/shard_map/ppermute | solution.py:94
  148.7 11.3 %collective-permute-start.4 = (bf16[1,16384]{1,0:T(2,128)(2,1)S(1)}, bf16[1,16384]{1,0:T(2,128)(2,1)S(1)}, u32[]{:S(2)}, u32[]{:S(2)}) collective-permute-start(bf16[1,16384]{1,0:T(2,128)(2,1)S(1)} %dynamic_slice.37), channel_id=1, source_target_pairs={{0,20},{4,16},{8,28},{12,24},{16,4},{20,0},{24,12},{28,8},{1,21},{... | collective-permute-start | bytes 98312 | tf_op jit(solution)/shard_map/ppermute | solution.py:94
  150.3 10.9 %collective-permute-start.5 = (bf16[1,16384]{1,0:T(2,128)(2,1)S(1)}, bf16[1,16384]{1,0:T(2,128)(2,1)S(1)}, u32[]{:S(2)}, u32[]{:S(2)}) collective-permute-start(bf16[1,16384]{1,0:T(2,128)(2,1)S(1)} %dynamic_slice.38), channel_id=1, source_target_pairs={{0,24},{4,28},{8,16},{12,20},{16,8},{20,12},{24,0},{28,4},{1,25},{... | collective-permute-start | bytes 98312 | tf_op jit(solution)/shard_map/ppermute | solution.py:94
  153.7 8.9 %collective-permute-start.6 = (bf16[1,16384]{1,0:T(2,128)(2,1)S(1)}, bf16[1,16384]{1,0:T(2,128)(2,1)S(1)}, u32[]{:S(2)}, u32[]{:S(2)}) collective-permute-start(bf16[1,16384]{1,0:T(2,128)(2,1)S(1)} %dynamic_slice.39), channel_id=1, source_target_pairs={{0,28},{4,24},{8,20},{12,16},{16,12},{20,8},{24,4},{28,0},{1,29},{... | collective-permute-start | bytes 98312 | tf_op jit(solution)/shard_map/ppermute | solution.py:94
  163.7 0.7 copy-start.7
  164.4 103.6 %all-reduce.2.cloned.1.call-start = ((), (), s32[]{:S(2)}) async-start(), calls=%async_computation.6 | async-start | bytes 262144 | tf_op jit(solution)/shard_map/psum | solution.py:106
  181.3 16.1 %copy-start.6 = (bf16[32,16384]{1,0:T(8,128)(2,1)S(1)}, bf16[32,16384]{1,0:T(8,128)(2,1)}, u32[]{:S(2)}) copy-start(bf16[32,16384]{1,0:T(8,128)(2,1)} %all-gather.8.cloned.1.call-done) | copy-start | bytes 3145732
  197.4 73.1 %copy-start.1 = (bf16[256,1024]{1,0:T(8,128)(2,1)S(1)}, bf16[256,1024]{1,0:T(8,128)(2,1)}, u32[]{:S(2)}) copy-start(bf16[256,1024]{1,0:T(8,128)(2,1)} %param.11) | copy-start | bytes 1572868
Sparse Core Ops, SparseCore 0:
  25.6 33.9 reduce-scatter.1
  61.1 22.5 all-gather.3
  85.2 22.5 all-gather.5
  164.5 16.6 all-gather.7
  197.5 70.4 all-reduce.1
